TPU v7x, 32 devices: a whole 2x2x4 slice. The times are simulated.
32 devices in a mesh: dp: 32 (over z, y, x, core).
Axes of the slice: x: 2, y: 2, z: 4, core: 2. Of those that a mesh axis runs over, the one named last changes fastest.
Arguments:
- features: bfloat16 [256, 128, 1024], P('dp'), may hold values from -16 to 16
- ln_gain: float32 [1024], replicated, may hold values from 0.5 to 1.5
- w_query: bfloat16 [1024, 1024], replicated, may hold values from -0.1875 to 0.1875
- w_key: bfloat16 [1024, 1024], replicated, may hold values from -0.1875 to 0.1875
- w_value: bfloat16 [1024, 1024], replicated, may hold values from -0.1875 to 0.1875
- w_out: bfloat16 [1024, 1024], replicated, may hold values from -0.1875 to 0.1875
- text_raw: bfloat16 [256, 1024], P('dp'), may hold values from -0.35 to 0.35
Outputs:
- loss: float32 [], replicated
- text_grad: float32 [256, 1024], P('dp')
- w_out_grad: bfloat16 [1024, 1024], replicated
All inputs are finite; a program needn't handle non-finite values.
Results may differ from a plain program's by a relative error of at most 0.009.
Values may be sent and summed in bfloat16 or wider, within the bound.
A program may use at most 128 MiB of HBM per device.

v0:
```python
import functools

import jax
import jax.numpy as jnp
from jax import lax
from jax.experimental import pallas as pl
from jax.experimental.pallas import tpu as pltpu
from jax.sharding import PartitionSpec as P

HEADS = 16
GROUP = 4

inv_temp = 1.0 / 0.07
attn_temp = 8.0
epsilon = 1e-06
log2e = 1.4426950408889634

F32 = jnp.float32
BF16 = jnp.bfloat16
NT = (((1,), (1,)), ((), ()))
TN = (((0,), (0,)), ((), ()))


MESH = pl.DeviceIdType.MESH


def target(n, i):
    return lax.rem(lax.axis_index("dp") + 2 * i, n)


def mate():
    me = lax.axis_index("dp")
    return me + 1 - 2 * lax.rem(me, 2)


def greet(n):
    barrier = pltpu.get_barrier_semaphore()

    def hello(i, _):
        pl.semaphore_signal(barrier, inc=1, device_id=(target(n, i),), device_id_type=MESH)
        return 0

    pl.semaphore_signal(barrier, inc=1, device_id=(mate(),), device_id_type=MESH)
    lax.fori_loop(1, n // 2, hello, 0)


class Share:
    def __init__(self, n, src, out, sems, own_sem):
        self.n, self.src, self.out, self.sems = n, src, out, sems
        self.half = n // 2
        self.own = pltpu.make_async_copy(src, out.at[lax.axis_index("dp")], own_sem)

    def direct(self, i):
        return pltpu.make_async_remote_copy(
            src_ref=self.src,
            dst_ref=self.out.at[lax.axis_index("dp")],
            send_sem=self.sems.at[0, i],
            recv_sem=self.sems.at[1, i],
            device_id=(target(self.n, i),),
            device_id_type=MESH,
        )

    def relay(self, i):
        slot = lax.rem(lax.axis_index("dp") - 2 * i + self.n, self.n)
        return pltpu.make_async_remote_copy(
            src_ref=self.out.at[slot],
            dst_ref=self.out.at[slot],
            send_sem=self.sems.at[2, i],
            recv_sem=self.sems.at[3, i],
            device_id=(mate(),),
            device_id_type=MESH,
        )

    def each(self, low, act):
        def step(i, _):
            act(i)
            return 0

        lax.fori_loop(low, self.half, step, 0)

    def start(self):
        self.own.start()
        self.each(1, lambda i: self.direct(i).start())

    def forward(self):
        self.own.wait()
        self.relay(0).start()

        def pass_on(i):
            self.direct(i).wait_recv()
            self.relay(i).start()

        self.each(1, pass_on)

    def finish(self):
        self.each(1, lambda i: self.direct(i).wait_send())

        def drain(i):
            self.relay(i).wait_send()
            self.relay(i).wait_recv()

        self.each(0, drain)


class LineShare:
    def __init__(self, n, lines, src, out, sems, own_sem):
        self.n, self.lines, self.src, self.out, self.sems = n, lines, src, out, sems
        self.plane = n // lines
        self.peers = self.plane // 2
        self.me = lax.axis_index("dp")
        self.spot = lax.rem(self.me, self.plane)
        self.own = pltpu.make_async_copy(src, out.at[self.me], own_sem)

    def block(self, j, k):
        owner = self.me - self.spot + lax.rem(self.spot - 2 * k + self.plane, self.plane)
        return self.out.at[lax.rem(owner - self.plane * j + self.n, self.n)]

    def copy(self, kind, j, k, src, dst, device):
        return pltpu.make_async_remote_copy(
            src_ref=src,
            dst_ref=dst,
            send_sem=self.sems.at[2 * kind, j, k],
            recv_sem=self.sems.at[2 * kind + 1, j, k],
            device_id=(device,),
            device_id_type=MESH,
        )

    def along(self, j):
        device = lax.rem(self.me + self.plane * j, self.n)
        return self.copy(0, j, 0, self.src, self.out.at[self.me], device)

    def across(self, j, k):
        device = self.me - self.spot + lax.rem(self.spot + 2 * k, self.plane)
        here = self.block(j, 0)
        return self.copy(1, j, k, self.src if j == 0 else here, here, device)

    def relay(self, j, k):
        here = self.block(j, k)
        return self.copy(2, j, k, here, here, mate())

    def each(self, low, act):
        def step(k, _):
            act(k)
            return 0

        lax.fori_loop(low, self.peers, step, 0)

    def run(self):
        self.own.start()
        for j in range(1, self.lines):
            self.along(j).start()
        self.each(1, lambda k: self.across(0, k).start())
        self.own.wait()
        self.relay(0, 0).start()
        for j in range(1, self.lines):
            self.along(j).wait_recv()
            self.each(1, lambda k: self.across(j, k).start())
            self.relay(j, 0).start()

        for j in range(self.lines):

            def pass_on(k):
                self.across(j, k).wait_recv()
                self.relay(j, k).start()

            self.each(1, pass_on)
        for j in range(1, self.lines):
            self.along(j).wait_send()
        for j in range(self.lines):
            self.each(1, lambda k: self.across(j, k).wait_send())

            def drain(k):
                self.relay(j, k).wait_send()
                self.relay(j, k).wait_recv()

            self.each(0, drain)


def line_count(n):
    return 4 if n % 8 == 0 else 1


def embed_kernel(
    n,
    x_hbm,
    gain_ref,
    wq_hbm,
    wk_hbm,
    wv_hbm,
    wo_hbm,
    text_ref,
    all_img,
    all_txt,
    msg_ref,
    txt_ref,
    xs,
    wqs,
    wks,
    wvs,
    wos,
    normed,
    qn,
    kn,
    pooled,
    zhi,
    zlo,
    xbar,
    x_sem,
    q_sem,
    k_sem,
    v_sem,
    o_sem,
    img_sems,
    txt_sems,
    own_sem,
):
    images, tokens, width = xs.shape
    groups = wqs.shape[0]
    cols = width // groups
    head = width // HEADS

    def x_copy(i):
        return pltpu.make_async_copy(x_hbm.at[i], xs.at[i], x_sem.at[i])

    def q_copy(g):
        return pltpu.make_async_copy(wq_hbm.at[:, pl.ds(g * cols, cols)], wqs.at[g], q_sem.at[g])

    def k_copy(g):
        return pltpu.make_async_copy(wk_hbm.at[:, pl.ds(g * cols, cols)], wks.at[g], k_sem.at[g])

    v_copy = pltpu.make_async_copy(wv_hbm, wvs, v_sem)
    o_copy = pltpu.make_async_copy(wo_hbm, wos, o_sem)
    for i in range(images):
        x_copy(i).start()
    for g in range(groups):
        q_copy(g).start()
        k_copy(g).start()
    v_copy.start()
    o_copy.start()

    greet(n)
    text32 = text_ref[...].astype(F32)
    txt_norm = jnp.sqrt(jnp.sum(text32 * text32, axis=1, keepdims=True) + epsilon)
    txt_ref[...] = (text32 / txt_norm).astype(BF16)
    txt_share = Share(n, txt_ref, all_txt, txt_sems, own_sem.at[0])
    img_share = LineShare(n, line_count(n), msg_ref, all_img, img_sems, own_sem.at[1])

    gain = gain_ref[...]
    block = 32

    def norm_image(i, _):
        x_copy(i).wait()

        def norm_block(b, acc):
            x = xs[i, pl.ds(b * block, block), :].astype(F32)
            center = x - jnp.mean(x, axis=-1, keepdims=True)
            spread = jnp.mean(center * center, axis=-1, keepdims=True)
            out = center * lax.rsqrt(spread + epsilon) * gain
            rows = pl.ds(pl.multiple_of(i * tokens + b * block, block), block)
            normed[rows, :] = out.astype(BF16)
            return acc + jnp.sum(x, axis=0, keepdims=True)

        total = lax.fori_loop(0, tokens // block, norm_block, jnp.zeros((1, width), F32), unroll=4)
        first = xs[i, pl.ds(0, 1), :].astype(F32)
        xbar[pl.ds(i, 1), :] = first + (total - first) / (tokens - 1)
        return 0

    norm_image(0, 0)
    pl.semaphore_wait(pltpu.get_barrier_semaphore(), n // 2)
    txt_share.start()
    lax.fori_loop(1, images, norm_image, 0)

    seg_row = lax.broadcasted_iota(jnp.int32, (cols, cols), 0) // head
    seg_col = lax.broadcasted_iota(jnp.int32, (cols, cols), 1) // head
    seg = jnp.where(seg_row == seg_col, 1.0, 0.0).astype(BF16)
    lane_head = lax.broadcasted_iota(jnp.int32, (tokens, cols), 1) // head
    coef = jnp.where(
        lax.broadcasted_iota(jnp.int32, (tokens, 1), 0) == 0, 1.0, 1.0 / (tokens - 1)
    ).astype(F32)

    def unit(proj):
        sq = jnp.dot((proj * proj).astype(BF16), seg, preferred_element_type=F32)
        return (proj * lax.rsqrt(sq + epsilon)).astype(BF16)

    def group_body(g, _):
        q_copy(g).wait()
        k_copy(g).wait()
        qn[...] = unit(jnp.dot(normed[...], wqs[g], preferred_element_type=F32))
        kn[...] = unit(jnp.dot(normed[...], wks[g], preferred_element_type=F32))

        def image_body(i, _):
            rows = pl.ds(pl.multiple_of(i * tokens, tokens), tokens)
            qi = qn[rows, :]
            ki = kn[rows, :]
            km = jnp.concatenate(
                [jnp.where(lane_head == h, ki, jnp.zeros_like(ki)) for h in range(cols // head)],
                axis=0,
            )
            s = lax.dot_general(qi, km, NT, preferred_element_type=F32)
            e = jnp.exp2(s * (attn_temp * log2e))
            for h in range(cols // head):
                eh = e[:, h * tokens : (h + 1) * tokens]
                scale = coef / jnp.sum(eh, axis=-1, keepdims=True)
                ph = jnp.sum(eh * scale, axis=0, keepdims=True)
                pooled[i, pl.ds(g * (cols // head) + h, 1), :] = ph
            return 0

        lax.fori_loop(0, images, image_body, 0, unroll=8)
        return 0

    lax.fori_loop(0, groups, group_body, 0)
    txt_share.forward()

    for i in range(images):
        p = pooled[i]
        hi = p.astype(BF16)
        lo = (p - hi.astype(F32)).astype(BF16)
        z2 = jnp.dot(
            jnp.concatenate([hi, lo], axis=0),
            normed[i * tokens : (i + 1) * tokens, :],
            preferred_element_type=F32,
        )
        z = z2[:HEADS] + z2[HEADS:]
        hi = z.astype(BF16)
        zhi[i * HEADS : (i + 1) * HEADS, :] = hi
        zlo[i * HEADS : (i + 1) * HEADS, :] = (z - hi.astype(F32)).astype(BF16)

    v_copy.wait()
    o_copy.wait()
    full = jnp.dot(zhi[...], wvs[...], preferred_element_type=F32) + jnp.dot(
        zlo[...], wvs[...], preferred_element_type=F32
    )
    own_head = lax.broadcasted_iota(jnp.int32, (HEADS, width), 0) == (
        lax.broadcasted_iota(jnp.int32, (HEADS, width), 1) // head
    )
    picked = [
        jnp.sum(
            jnp.where(own_head, full[i * HEADS : (i + 1) * HEADS, :], 0.0), axis=0, keepdims=True
        )
        for i in range(images)
    ]
    abar = jnp.concatenate(picked, axis=0).astype(BF16)
    emb = xbar[...] + jnp.dot(abar, wos[...], preferred_element_type=F32)
    emb_norm = jnp.sqrt(jnp.sum(emb * emb, axis=1, keepdims=True) + epsilon)
    n0 = emb_norm.astype(BF16).astype(F32)
    n1 = (emb_norm - n0).astype(BF16).astype(F32)
    n2 = emb_norm - n0 - n1
    lane = lax.broadcasted_iota(jnp.int32, (images, 128), 1)
    tail = jnp.where(lane == 0, n0, jnp.where(lane == 1, n1, jnp.where(lane == 2, n2, 0.0)))
    msg_ref[:, 0:width] = (emb / emb_norm).astype(BF16)
    msg_ref[:, width : 2 * width] = abar
    msg_ref[:, 2 * width :] = tail.astype(BF16)
    img_share.run()
    txt_share.finish()


def embed(features, ln_gain, w_query, w_key, w_value, w_out, text_raw, n):
    images, tokens, width = features.shape
    groups = HEADS // GROUP
    cols = width // groups
    hbm = pl.BlockSpec(memory_space=pl.ANY)
    vmem = pl.BlockSpec(memory_space=pltpu.VMEM)
    return pl.pallas_call(
        functools.partial(embed_kernel, n),
        out_shape=(
            jax.ShapeDtypeStruct((n, images, 2 * width + 128), BF16),
            jax.ShapeDtypeStruct((n, images, width), BF16),
        ),
        in_specs=[hbm, vmem, hbm, hbm, hbm, hbm, vmem],
        out_specs=(vmem, vmem),
        scratch_shapes=[
            pltpu.VMEM((images, 2 * width + 128), BF16),
            pltpu.VMEM((images, width), BF16),
            pltpu.VMEM((images, tokens, width), BF16),
            pltpu.VMEM((groups, width, cols), BF16),
            pltpu.VMEM((groups, width, cols), BF16),
            pltpu.VMEM((width, width), BF16),
            pltpu.VMEM((width, width), BF16),
            pltpu.VMEM((images * tokens, width), BF16),
            pltpu.VMEM((images * tokens, cols), BF16),
            pltpu.VMEM((images * tokens, cols), BF16),
            pltpu.VMEM((images, HEADS, tokens), F32),
            pltpu.VMEM((images * HEADS, width), BF16),
            pltpu.VMEM((images * HEADS, width), BF16),
            pltpu.VMEM((images, width), F32),
            pltpu.SemaphoreType.DMA((images,)),
            pltpu.SemaphoreType.DMA((groups,)),
            pltpu.SemaphoreType.DMA((groups,)),
            pltpu.SemaphoreType.DMA,
            pltpu.SemaphoreType.DMA,
            pltpu.SemaphoreType.DMA((6, line_count(n), n // line_count(n) // 2)),
            pltpu.SemaphoreType.DMA((4, n // 2)),
            pltpu.SemaphoreType.DMA((2,)),
        ],
        compiler_params=pltpu.CompilerParams(collective_id=0, has_side_effects=True),
        name="embed",
    )(features, ln_gain.reshape(1, width), w_query, w_key, w_value, w_out, text_raw)


def loss_kernel(all_ref, txt_all_ref, text_ref, me_ref, loss_ref, text_grad_ref, w_grad_ref):
    total = all_ref.shape[0]
    images, width = text_ref.shape
    img = all_ref[:, 0:width]
    txt = txt_all_ref[...]
    logits = inv_temp * lax.dot_general(img, txt, NT, preferred_element_type=F32)
    e = jnp.exp(logits)
    flipped = jnp.exp(inv_temp * lax.dot_general(txt, img, NT, preferred_element_type=F32))
    rowsum = jnp.sum(e, axis=1, keepdims=True)
    colsum = jnp.sum(e, axis=0, keepdims=True)
    rowsum_flat = jnp.sum(flipped, axis=0, keepdims=True)
    eye = lax.broadcasted_iota(jnp.int32, (total, total), 0) == lax.broadcasted_iota(
        jnp.int32, (total, total), 1
    )
    diag = jnp.sum(jnp.where(eye, logits, 0.0))
    loss = (jnp.sum(jnp.log(rowsum_flat)) + jnp.sum(jnp.log(colsum)) - 2.0 * diag) / (2.0 * total)
    loss_ref[0, 0] = loss

    delta = 0.5 * (e / rowsum + e / colsum) - jnp.where(eye, 1.0, 0.0)
    grad_img = inv_temp * jnp.dot(delta.astype(BF16), txt, preferred_element_type=F32)
    norms = all_ref[:, 2 * width :].astype(F32)
    emb_norm = jnp.sum(norms, axis=1, keepdims=True)
    img32 = img.astype(F32)
    emb_grad = (grad_img - img32 * jnp.sum(img32 * grad_img, axis=1, keepdims=True)) / emb_norm
    hi = emb_grad.astype(BF16)
    lo = (emb_grad - hi.astype(F32)).astype(BF16)
    abar = all_ref[:, width : 2 * width]
    w_grad = lax.dot_general(abar, hi, TN, preferred_element_type=F32) + lax.dot_general(
        abar, lo, TN, preferred_element_type=F32
    )
    w_grad_ref[...] = w_grad.astype(BF16)

    text32 = text_ref[...].astype(F32)
    txt_norm = jnp.sqrt(jnp.sum(text32 * text32, axis=1, keepdims=True) + epsilon)
    txt_f = text32 / txt_norm
    own = inv_temp * lax.dot_general(
        txt_f.astype(BF16), img, NT, preferred_element_type=F32
    )
    own_e = jnp.exp(own)
    own_sum = jnp.sum(own_e, axis=1, keepdims=True)
    col = lax.broadcasted_iota(jnp.int32, (images, total), 1)
    row = lax.broadcasted_iota(jnp.int32, (images, total), 0) + me_ref[0] * images
    own_delta = 0.5 * (own_e / rowsum_flat + own_e / own_sum) - jnp.where(col == row, 1.0, 0.0)
    grad_txt = inv_temp * jnp.dot(own_delta.astype(BF16), img, preferred_element_type=F32)
    text_grad_ref[...] = (
        grad_txt - txt_f * jnp.sum(txt_f * grad_txt, axis=1, keepdims=True)
    ) / txt_norm


def finish(all_img, all_txt, text_raw):
    images, width = text_raw.shape
    vmem = pl.BlockSpec(memory_space=pltpu.VMEM)
    smem = pl.BlockSpec(memory_space=pltpu.SMEM)
    me = lax.axis_index("dp").astype(jnp.int32).reshape(1)
    loss, text_grad, w_grad = pl.pallas_call(
        loss_kernel,
        out_shape=(
            jax.ShapeDtypeStruct((1, 1), F32),
            jax.ShapeDtypeStruct((images, width), F32),
            jax.ShapeDtypeStruct((width, width), BF16),
        ),
        in_specs=[vmem, vmem, vmem, smem],
        out_specs=(smem, vmem, vmem),
        name="finish",
    )(all_img, all_txt, text_raw, me)
    return loss.reshape(()), text_grad, w_grad


def solution(mesh):
    n = mesh.shape["dp"]

    def local(features, ln_gain, w_query, w_key, w_value, w_out, text_raw):
        all_img, all_txt = embed(
            features, ln_gain, w_query, w_key, w_value, w_out, text_raw, n
        )
        pairs = n * text_raw.shape[0]
        return finish(all_img.reshape(pairs, -1), all_txt.reshape(pairs, -1), text_raw)

    placed = (P("dp", None, None), P(), P(), P(), P(), P(), P("dp", None))
    return jax.shard_map(
        local, mesh=mesh, in_specs=placed, out_specs=(P(), P("dp", None), P()), check_vma=False
    )
```

profile of v0, /device:TPU:0, one launch (start us, length us, event | category | flops | bytes accessed | tf_op | source)
XLA Modules:
  0.0 41.7 jit_solution(18260796848905711463)
XLA Ops:
  0.6 36.1 %embed.1 = (bf16[32,8,2176]{2,1,0:T(8,128)(2,1)}, bf16[32,8,1024]{2,1,0:T(8,128)(2,1)}) custom-call(bf16[8,128,1024]{2,1,0:T(8,128)(2,1)} %x_hbm.1, f32[1,1024]{1,0:T(1,128)} %bitcast.7, bf16[1024,1024]{1,0:T(8,128)(2,1)} %wq_hbm.1, bf16[1024,1024]{1,0:T(8,128)(2,1)} %wk_hbm.1, bf16[1024,1024]{1,0:T(8,128)(2,1)} %wv_hbm.1, bf16[1024,1024]{1,0:T(8,128)(2,1)} %wo_hbm.1, ...), custom_call_target="tpu_custom_call" | custom-call | tf_op jit(solution)/shard_map/embed/pallas_call | solution.py:363
  36.8 5.0 %finish.1 = (f32[1,1]{1,0:T(1,128)}, f32[8,1024]{1,0:T(8,128)}, bf16[1024,1024]{1,0:T(8,128)(2,1)}) custom-call(bf16[256,2176]{1,0:T(8,128)(2,1)} %bitcast.5, bf16[256,1024]{1,0:T(8,128)(2,1)} %bitcast.6, bf16[8,1024]{1,0:T(8,128)(2,1)} %text_ref.3, s32[1]{0:T(128)} %bitcast.3.me_ref), custom_call_target="tpu_custom_call" | custom-call | tf_op jit(solution)/shard_map/finish/pallas_call | solution.py:454
where the time goes:
time: 42 us; the launch traced here: 41.7 us
  Pallas kernels  41.1 us (98%)
  between operations  0.64 us (2%)
    pallas_call x1, Pallas kernels, embed(): pl.pallas_call(functools.partial(embed_kernel, n), out_shape=(jax.ShapeDt...  36.1 us
    pallas_call x1, Pallas kernels, finish(): pl.pallas_call(loss_kernel, out_shape=(jax.ShapeDtypeStruct((1, 1), F32),...  4.99 us

commit v1 on v0

--- a/solution.py
+++ b/solution.py
@@ -9,6 +9,7 @@
 
 HEADS = 16
 GROUP = 4
+BLOCKS = 2
 
 inv_temp = 1.0 / 0.07
 attn_temp = 8.0
@@ -194,13 +195,12 @@
     msg_ref,
     txt_ref,
     xs,
-    wqs,
-    wks,
+    wqks,
     wvs,
     wos,
     normed,
-    qn,
-    kn,
+    qkn0,
+    qkn1,
     pooled,
     zhi,
     zlo,
@@ -215,7 +215,7 @@
     own_sem,
 ):
     images, tokens, width = xs.shape
-    groups = wqs.shape[0]
+    groups = wqks.shape[0]
     cols = width // groups
     head = width // HEADS
 
@@ -223,10 +223,10 @@
         return pltpu.make_async_copy(x_hbm.at[i], xs.at[i], x_sem.at[i])
 
     def q_copy(g):
-        return pltpu.make_async_copy(wq_hbm.at[:, pl.ds(g * cols, cols)], wqs.at[g], q_sem.at[g])
+        return pltpu.make_async_copy(wq_hbm.at[:, pl.ds(g * cols, cols)], wqks.at[g, :, pl.ds(0, cols)], q_sem.at[g])
 
     def k_copy(g):
-        return pltpu.make_async_copy(wk_hbm.at[:, pl.ds(g * cols, cols)], wks.at[g], k_sem.at[g])
+        return pltpu.make_async_copy(wk_hbm.at[:, pl.ds(g * cols, cols)], wqks.at[g, :, pl.ds(cols, cols)], k_sem.at[g])
 
     v_copy = pltpu.make_async_copy(wv_hbm, wvs, v_sem)
     o_copy = pltpu.make_async_copy(wo_hbm, wos, o_sem)
@@ -247,6 +247,7 @@
 
     gain = gain_ref[...]
     block = 32
+    blocks = BLOCKS
 
     def norm_image(i, _):
         x_copy(i).wait()
@@ -265,15 +266,14 @@
         xbar[pl.ds(i, 1), :] = first + (total - first) / (tokens - 1)
         return 0
 
-    norm_image(0, 0)
-    pl.semaphore_wait(pltpu.get_barrier_semaphore(), n // 2)
-    txt_share.start()
-    lax.fori_loop(1, images, norm_image, 0)
+    lax.fori_loop(0, images, norm_image, 0)
 
     seg_row = lax.broadcasted_iota(jnp.int32, (cols, cols), 0) // head
     seg_col = lax.broadcasted_iota(jnp.int32, (cols, cols), 1) // head
     seg = jnp.where(seg_row == seg_col, 1.0, 0.0).astype(BF16)
-    lane_head = lax.broadcasted_iota(jnp.int32, (tokens, cols), 1) // head
+    lanes = 128
+    per = lanes // head
+    lane_head = lax.broadcasted_iota(jnp.int32, (tokens, lanes), 1) // head
     coef = jnp.where(
         lax.broadcasted_iota(jnp.int32, (tokens, 1), 0) == 0, 1.0, 1.0 / (tokens - 1)
     ).astype(F32)
@@ -282,33 +282,48 @@
         sq = jnp.dot((proj * proj).astype(BF16), seg, preferred_element_type=F32)
         return (proj * lax.rsqrt(sq + epsilon)).astype(BF16)
 
-    def group_body(g, _):
-        q_copy(g).wait()
-        k_copy(g).wait()
-        qn[...] = unit(jnp.dot(normed[...], wqs[g], preferred_element_type=F32))
-        kn[...] = unit(jnp.dot(normed[...], wks[g], preferred_element_type=F32))
-
-        def image_body(i, _):
-            rows = pl.ds(pl.multiple_of(i * tokens, tokens), tokens)
-            qi = qn[rows, :]
-            ki = kn[rows, :]
+    def project(g, b):
+        rows = pl.ds(b * (images * tokens // blocks), images * tokens // blocks)
+        proj = jnp.dot(normed[rows, :], wqks[g], preferred_element_type=F32)
+        qkn = qkns[g % 2]
+        qkn[rows, 0:cols] = unit(proj[:, 0:cols])
+        qkn[rows, cols : 2 * cols] = unit(proj[:, cols : 2 * cols])
+
+    def attend(g, i):
+        rows = pl.ds(i * tokens, tokens)
+        qkn = qkns[g % 2]
+        for pair in range(cols // lanes):
+            lo = pair * lanes
+            qi = qkn[rows, lo : lo + lanes]
+            ki = qkn[rows, cols + lo : cols + lo + lanes]
             km = jnp.concatenate(
-                [jnp.where(lane_head == h, ki, jnp.zeros_like(ki)) for h in range(cols // head)],
+                [jnp.where(lane_head == h, ki, jnp.zeros_like(ki)) for h in range(per)],
                 axis=0,
             )
             s = lax.dot_general(qi, km, NT, preferred_element_type=F32)
             e = jnp.exp2(s * (attn_temp * log2e))
-            for h in range(cols // head):
+            for h in range(per):
                 eh = e[:, h * tokens : (h + 1) * tokens]
                 scale = coef / jnp.sum(eh, axis=-1, keepdims=True)
                 ph = jnp.sum(eh * scale, axis=0, keepdims=True)
-                pooled[i, pl.ds(g * (cols // head) + h, 1), :] = ph
-            return 0
-
-        lax.fori_loop(0, images, image_body, 0, unroll=8)
-        return 0
-
-    lax.fori_loop(0, groups, group_body, 0)
+                at = g * (cols // head) + pair * per + h
+                pooled[i, at : at + 1, :] = ph
+
+    qkns = (qkn0, qkn1)
+    for g in range(groups + 1):
+        if g < groups:
+            q_copy(g).wait()
+            k_copy(g).wait()
+        if g == 1:
+            pl.semaphore_wait(pltpu.get_barrier_semaphore(), n // 2)
+            txt_share.start()
+        for b in range(blocks):
+            if g > 0:
+                for i in range(b * images // blocks, (b + 1) * images // blocks):
+                    attend(g - 1, i)
+            if g < groups:
+                project(g, b)
+
     txt_share.forward()
 
     for i in range(images):
@@ -372,13 +387,12 @@
             pltpu.VMEM((images, 2 * width + 128), BF16),
             pltpu.VMEM((images, width), BF16),
             pltpu.VMEM((images, tokens, width), BF16),
-            pltpu.VMEM((groups, width, cols), BF16),
-            pltpu.VMEM((groups, width, cols), BF16),
+            pltpu.VMEM((groups, width, 2 * cols), BF16),
             pltpu.VMEM((width, width), BF16),
             pltpu.VMEM((width, width), BF16),
             pltpu.VMEM((images * tokens, width), BF16),
-            pltpu.VMEM((images * tokens, cols), BF16),
-            pltpu.VMEM((images * tokens, cols), BF16),
+            pltpu.VMEM((images * tokens, 2 * cols), BF16),
+            pltpu.VMEM((images * tokens, 2 * cols), BF16),
             pltpu.VMEM((images, HEADS, tokens), F32),
             pltpu.VMEM((images * HEADS, width), BF16),
             pltpu.VMEM((images * HEADS, width), BF16),

time: 42 us -> 36.8 us (0.88)
  Pallas kernels: 41.1 us -> 35.8 us
    pallas_call x1, Pallas kernels: 36.1 us -> 30.8 us  [embed(): pl.pallas_call(functools.partial(embed_kernel, n), out_shape=(jax.ShapeDt...]
where the time goes in v1:
time: 36.8 us; the launch traced here: 36.5 us
  Pallas kernels  35.8 us (97%)
  between operations  0.64 us (2%)
    pallas_call x1, Pallas kernels, embed(): pl.pallas_call(functools.partial(embed_kernel, n), out_shape=(jax.ShapeDt...  30.8 us
    pallas_call x1, Pallas kernels, finish(): pl.pallas_call(loss_kernel, out_shape=(jax.ShapeDtypeStruct((1, 1), F32),...  4.99 us

profile of v1, /device:TPU:0, one launch (start us, length us, event | category | flops | bytes accessed | tf_op | source)
XLA Modules:
  0.0 36.5 jit_solution(10067127407262057172)
XLA Ops:
  0.6 30.8 %embed.1 = (bf16[32,8,2176]{2,1,0:T(8,128)(2,1)}, bf16[32,8,1024]{2,1,0:T(8,128)(2,1)}) custom-call(bf16[8,128,1024]{2,1,0:T(8,128)(2,1)} %x_hbm.1, f32[1,1024]{1,0:T(1,128)} %bitcast.7, bf16[1024,1024]{1,0:T(8,128)(2,1)} %wq_hbm.1, bf16[1024,1024]{1,0:T(8,128)(2,1)} %wk_hbm.1, bf16[1024,1024]{1,0:T(8,128)(2,1)} %wv_hbm.1, bf16[1024,1024]{1,0:T(8,128)(2,1)} %wo_hbm.1, ...), custom_call_target="tpu_custom_call" | custom-call | tf_op jit(solution)/shard_map/embed/pallas_call | solution.py:378
  31.5 5.0 %finish.1 = (f32[1,1]{1,0:T(1,128)}, f32[8,1024]{1,0:T(8,128)}, bf16[1024,1024]{1,0:T(8,128)(2,1)}) custom-call(bf16[256,2176]{1,0:T(8,128)(2,1)} %bitcast.5, bf16[256,1024]{1,0:T(8,128)(2,1)} %bitcast.6, bf16[8,1024]{1,0:T(8,128)(2,1)} %text_ref.3, s32[1]{0:T(128)} %bitcast.3.me_ref), custom_call_target="tpu_custom_call" | custom-call | tf_op jit(solution)/shard_map/finish/pallas_call | solution.py:468

commit v2 on v1

v2 whole, which is shorter than its diff:
```python
import functools

import jax
import jax.numpy as jnp
from jax import lax
from jax.experimental import pallas as pl
from jax.experimental.pallas import tpu as pltpu
from jax.sharding import PartitionSpec as P

HEADS = 16
GROUP = 4
BLOCKS = 2
SLOTS = 8

inv_temp = 1.0 / 0.07
attn_temp = 8.0
epsilon = 1e-06
log2e = 1.4426950408889634

F32 = jnp.float32
BF16 = jnp.bfloat16
NT = (((1,), (1,)), ((), ()))
TN = (((0,), (0,)), ((), ()))


MESH = pl.DeviceIdType.MESH


def target(n, i):
    return lax.rem(lax.axis_index("dp") + 2 * i, n)


def mate():
    me = lax.axis_index("dp")
    return me + 1 - 2 * lax.rem(me, 2)


def greet(n):
    barrier = pltpu.get_barrier_semaphore()

    def hello(i, _):
        pl.semaphore_signal(barrier, inc=1, device_id=(target(n, i),), device_id_type=MESH)
        return 0

    pl.semaphore_signal(barrier, inc=1, device_id=(mate(),), device_id_type=MESH)
    lax.fori_loop(1, n // 2, hello, 0)


def each(low, high, act):
    def step(i, _):
        act(i)
        return 0

    lax.fori_loop(low, high, step, 0)


def remote(src, dst, sems, kind, device):
    return pltpu.make_async_remote_copy(
        src_ref=src,
        dst_ref=dst,
        send_sem=sems.at[2 * kind],
        recv_sem=sems.at[2 * kind + 1],
        device_id=(device,),
        device_id_type=MESH,
    )


class Exchange:
    def __init__(self, n, ref, sems):
        self.n, self.ref, self.sems = n, ref, sems
        self.me = lax.axis_index("dp")
        self.half = n // 2

    def own(self):
        return self.ref.at[self.me]

    def several(self, kind, count):
        blocks = self.ref.at[pl.ds(0, count)]
        return remote(blocks, blocks, self.sems, kind, mate())

    def relay(self):
        parity = lax.rem(self.me, 2)
        blocks = self.ref.reshape(self.half, 2, *self.ref.shape[1:]).at[:, parity]
        return remote(blocks, blocks, self.sems, self.last, mate())

    def forward(self):
        self.several(*self.counts[-1]).wait_recv()
        self.relay().start()

    def arrive(self):
        self.relay().wait_recv()

    def drain(self):
        for kind, count in self.counts:
            self.several(kind, count).wait_send()
        self.relay().wait_send()


class Share(Exchange):
    last = 1

    def __init__(self, n, ref, sems):
        super().__init__(n, ref, sems)
        self.counts = ((0, self.half - 1),)

    def start(self):
        own = self.own()
        each(1, self.half, lambda i: remote(own, own, self.sems, 0, target(self.n, i)).start())


class LineShare(Exchange):
    last = 2

    def __init__(self, n, ref, sems):
        super().__init__(n, ref, sems)
        self.lines = line_count(n)
        self.plane = n // self.lines
        self.peers = self.plane // 2
        self.spot = lax.rem(self.me, self.plane)
        self.counts = ((0, self.lines - 1), (1, self.lines * (self.peers - 1)))

    def across(self, j):
        block = self.ref.at[lax.rem(self.me - self.plane * j + self.n, self.n)]

        def send(k):
            device = self.me - self.spot + lax.rem(self.spot + 2 * k, self.plane)
            remote(block, block, self.sems, 1, device).start()

        each(1, self.peers, send)

    def start(self):
        own = self.own()
        for j in range(1, self.lines):
            remote(own, own, self.sems, 0, lax.rem(self.me + self.plane * j, self.n)).start()
        self.across(0)

    def spread(self):
        self.several(*self.counts[0]).wait_recv()
        for j in range(1, self.lines):
            self.across(j)


def line_count(n):
    return 4 if n % 8 == 0 else 1


def embed_kernel(
    n,
    x_hbm,
    gain_hbm,
    wq_hbm,
    wk_hbm,
    wv_hbm,
    wo_hbm,
    text_hbm,
    all_txt,
    abar0,
    abar1,
    abar2,
    emb_ref,
    text_ref,
    xs,
    gain_ref,
    wqks,
    wvs,
    wos,
    normed,
    qkn0,
    qkn1,
    pooled,
    zs,
    xbar,
    all_xbar,
    x_sem,
    q_sem,
    k_sem,
    w_sem,
    share_sems,
):
    images, tokens, width = xs.shape
    groups = wqks.shape[0]
    cols = width // groups
    head = width // HEADS
    me = lax.axis_index("dp")
    abars = (abar0, abar1, abar2)

    def x_copy(i):
        return pltpu.make_async_copy(x_hbm.at[i], xs.at[i], x_sem.at[i])

    def q_copy(g):
        return pltpu.make_async_copy(
            wq_hbm.at[:, pl.ds(g * cols, cols)], wqks.at[g, :, pl.ds(0, cols)], q_sem.at[g]
        )

    def k_copy(g):
        return pltpu.make_async_copy(
            wk_hbm.at[:, pl.ds(g * cols, cols)], wqks.at[g, :, pl.ds(cols, cols)], k_sem.at[g]
        )

    v_copy = pltpu.make_async_copy(wv_hbm, wvs, w_sem.at[0])
    o_copy = pltpu.make_async_copy(wo_hbm, wos, w_sem.at[1])
    gain_copy = pltpu.make_async_copy(gain_hbm, gain_ref, w_sem.at[2])
    text_copy = pltpu.make_async_copy(text_hbm, text_ref, w_sem.at[3])
    gain_copy.start()
    for i in range(images):
        x_copy(i).start()
    text_copy.start()
    greet(n)
    for g in range(groups):
        q_copy(g).start()
        k_copy(g).start()
    v_copy.start()
    o_copy.start()

    txt_share = LineShare(n, all_txt, share_sems.at[0])
    xbar_share = LineShare(n, all_xbar, share_sems.at[1])

    pooled[...] = jnp.zeros_like(pooled)
    gain_copy.wait()
    gain = gain_ref[...]
    block = 32

    def norm_image(i, _):
        x_copy(i).wait()

        def norm_block(b, acc):
            x = xs[i, pl.ds(b * block, block), :].astype(F32)
            center = x - jnp.mean(x, axis=-1, keepdims=True)
            spread = jnp.mean(center * center, axis=-1, keepdims=True)
            out = center * lax.rsqrt(spread + epsilon) * gain
            rows = pl.ds(pl.multiple_of(i * tokens + b * block, block), block)
            normed[rows, :] = out.astype(BF16)
            return acc + jnp.sum(x, axis=0, keepdims=True)

        total = lax.fori_loop(0, tokens // block, norm_block, jnp.zeros((1, width), F32), unroll=4)
        first = xs[i, pl.ds(0, 1), :].astype(F32)
        xbar[pl.ds(i, 1), :] = first + (total - first) / (tokens - 1)
        return 0

    lax.fori_loop(0, images, norm_image, 0)
    all_xbar[me] = xbar[...].astype(BF16)
    text_copy.wait()
    text32 = text_ref[...].astype(F32)
    txt_norm = jnp.sqrt(jnp.sum(text32 * text32, axis=1, keepdims=True) + epsilon)
    all_txt[me] = (text32 / txt_norm).astype(BF16)

    seg_row = lax.broadcasted_iota(jnp.int32, (cols, cols), 0) // head
    seg_col = lax.broadcasted_iota(jnp.int32, (cols, cols), 1) // head
    seg = jnp.where(seg_row == seg_col, 1.0, 0.0).astype(BF16)
    lanes = 128
    per = lanes // head
    lane_head = lax.broadcasted_iota(jnp.int32, (tokens, lanes), 1) // head
    coef = jnp.where(
        lax.broadcasted_iota(jnp.int32, (tokens, 1), 0) == 0, 1.0, 1.0 / (tokens - 1)
    ).astype(F32)

    def unit(proj):
        sq = jnp.dot((proj * proj).astype(BF16), seg, preferred_element_type=F32)
        return (proj * lax.rsqrt(sq + epsilon)).astype(BF16)

    qkns = (qkn0, qkn1)

    def project(g, b):
        rows = pl.ds(b * (images * tokens // BLOCKS), images * tokens // BLOCKS)
        proj = jnp.dot(normed[rows, :], wqks[g], preferred_element_type=F32)
        qkn = qkns[g % 2]
        qkn[rows, 0:cols] = unit(proj[:, 0:cols])
        qkn[rows, cols : 2 * cols] = unit(proj[:, cols : 2 * cols])

    def attend(g, i):
        rows = pl.ds(i * tokens, tokens)
        qkn = qkns[g % 2]
        for pair in range(cols // lanes):
            lo = pair * lanes
            qi = qkn[rows, lo : lo + lanes]
            ki = qkn[rows, cols + lo : cols + lo + lanes]
            km = jnp.concatenate(
                [jnp.where(lane_head == h, ki, jnp.zeros_like(ki)) for h in range(per)],
                axis=0,
            )
            s = lax.dot_general(qi, km, NT, preferred_element_type=F32)
            e = jnp.exp2(s * (attn_temp * log2e))
            for h in range(per):
                eh = e[:, h * tokens : (h + 1) * tokens]
                scale = coef / jnp.sum(eh, axis=-1, keepdims=True)
                ph = jnp.sum(eh * scale, axis=0, keepdims=True)
                at = g * SLOTS + pair * per + h
                pooled[i, at : at + 1, :] = ph

    def weigh(low, high):
        rows = SLOTS * (high - low)
        wide = cols * (high - low)
        for i in range(images):
            p = pooled[i, low * SLOTS : high * SLOTS, :]
            hi = p.astype(BF16)
            lo = (p - hi.astype(F32)).astype(BF16)
            z2 = jnp.dot(
                jnp.concatenate([hi, lo], axis=0),
                normed[i * tokens : (i + 1) * tokens, :],
                preferred_element_type=F32,
            )
            z = z2[:rows] + z2[rows:]
            hi = z.astype(BF16)
            zs[0, i * rows : (i + 1) * rows, :] = hi
            zs[1, i * rows : (i + 1) * rows, :] = (z - hi.astype(F32)).astype(BF16)
        wv = wvs[:, low * cols : high * cols]
        full = jnp.dot(zs[0, : images * rows, :], wv, preferred_element_type=F32) + jnp.dot(
            zs[1, : images * rows, :], wv, preferred_element_type=F32
        )
        slot = lax.broadcasted_iota(jnp.int32, (rows, wide), 0)
        owner = lax.broadcasted_iota(jnp.int32, (rows, wide), 1) // head
        keep = slot == owner // GROUP * SLOTS + owner % GROUP
        picked = [
            jnp.sum(
                jnp.where(keep, full[i * rows : (i + 1) * rows, :], 0.0), axis=0, keepdims=True
            )
            for i in range(images)
        ]
        return jnp.concatenate(picked, axis=0).astype(BF16)

    early, late, last = groups // 2, groups - 1, groups
    shares = [Share(n, part, share_sems.at[2 + c]) for c, part in enumerate(abars)]
    for g in range(groups + 1):
        if g < groups:
            q_copy(g).wait()
            k_copy(g).wait()
        if g == 1:
            pl.semaphore_wait(pltpu.get_barrier_semaphore(), n // 2)
            txt_share.start()
            xbar_share.start()
        if g == early + 1:
            txt_share.spread()
            v_copy.wait()
            abars[0][me] = weigh(0, early)
            shares[0].start()
        if g == groups:
            xbar_share.spread()
            abars[1][me] = weigh(early, late)
        for b in range(BLOCKS):
            if g > 0:
                for i in range(b * images // BLOCKS, (b + 1) * images // BLOCKS):
                    attend(g - 1, i)
            if g < groups:
                project(g, b)
    shares[1].start()
    abars[2][me] = weigh(late, last)
    shares[2].start()
    txt_share.forward()
    xbar_share.forward()
    shares[0].forward()
    shares[1].forward()
    xbar_share.arrive()
    shares[0].arrive()
    o_copy.wait()

    total = n * images
    chunk = min(total, 256)
    part = chunk // images

    def join(ref, r):
        return ref[r * part : (r + 1) * part].reshape(chunk, ref.shape[-1])

    def out_part(r, c, low, high):
        w = wos[low * cols : high * cols, :]
        return jnp.dot(join(abars[c], r), w, preferred_element_type=F32)

    for r in range(total // chunk):
        emb = join(all_xbar, r).astype(F32) + out_part(r, 0, 0, early)
        emb_ref[r * chunk : (r + 1) * chunk, :] = emb
    shares[2].forward()
    txt_share.arrive()
    shares[1].arrive()
    for share in (txt_share, xbar_share, *shares):
        if share is not shares[2]:
            share.drain()
    shares[2].arrive()
    for r in range(total // chunk):
        emb_ref[r * chunk : (r + 1) * chunk, :] += out_part(r, 1, early, late) + out_part(
            r, 2, late, last
        )
    shares[2].drain()


def embed(features, ln_gain, w_query, w_key, w_value, w_out, text_raw, n):
    images, tokens, width = features.shape
    groups = HEADS // GROUP
    cols = width // groups
    hbm = pl.BlockSpec(memory_space=pl.ANY)
    vmem = pl.BlockSpec(memory_space=pltpu.VMEM)
    args = (features, ln_gain.reshape(1, width), w_query, w_key, w_value, w_out, text_raw)
    args = [pltpu.with_memory_space_constraint(a, pltpu.HBM) for a in args]
    return pl.pallas_call(
        functools.partial(embed_kernel, n),
        out_shape=(
            pltpu.VMEM((n, images, width), BF16),
            pltpu.VMEM((n, images, width // 2), BF16),
            pltpu.VMEM((n, images, width // 4), BF16),
            pltpu.VMEM((n, images, width // 4), BF16),
            pltpu.VMEM((n * images, width), F32),
            pltpu.VMEM((images, width), BF16),
        ),
        in_specs=[hbm] * 7,
        out_specs=(vmem,) * 6,
        scratch_shapes=[
            pltpu.VMEM((images, tokens, width), BF16),
            pltpu.VMEM((1, width), F32),
            pltpu.VMEM((groups, width, 2 * cols), BF16),
            pltpu.VMEM((width, width), BF16),
            pltpu.VMEM((width, width), BF16),
            pltpu.VMEM((images * tokens, width), BF16),
            pltpu.VMEM((images * tokens, 2 * cols), BF16),
            pltpu.VMEM((images * tokens, 2 * cols), BF16),
            pltpu.VMEM((images, SLOTS * groups, tokens), F32),
            pltpu.VMEM((2, images * SLOTS * groups, width), BF16),
            pltpu.VMEM((images, width), F32),
            pltpu.VMEM((n, images, width), BF16),
            pltpu.SemaphoreType.DMA((images,)),
            pltpu.SemaphoreType.DMA((groups,)),
            pltpu.SemaphoreType.DMA((groups,)),
            pltpu.SemaphoreType.DMA((4,)),
            pltpu.SemaphoreType.DMA((5, 6)),
        ],
        compiler_params=pltpu.CompilerParams(
            collective_id=0, has_side_effects=True, vmem_limit_bytes=40 * 2**20
        ),
        name="embed",
    )(*args)


def loss_kernel(
    txt_ref, abar0, abar1, abar2, emb_ref, text_ref, loss_ref, text_grad_ref, w_hbm, img_s, grad_s, w_s, w_sem
):
    total, width = emb_ref.shape
    images = text_ref.shape[0]
    chunk = min(total, 256)
    chunks = [slice(r, r + chunk) for r in range(0, total, chunk)]

    def eye(r):
        row = lax.broadcasted_iota(jnp.int32, (chunk, total), 0) + r.start
        return row == lax.broadcasted_iota(jnp.int32, (chunk, total), 1)

    txt = txt_ref[...]
    invs, es, rowsums = [], [], []
    colsum = rowsum_flat = jnp.zeros((1, total), F32)
    diag = jnp.zeros((1, total), F32)
    for r in chunks:
        emb = emb_ref[r, :]
        inv = lax.rsqrt(jnp.sum(emb * emb, axis=1, keepdims=True) + epsilon)
        img = (emb * inv).astype(BF16)
        img_s[r, :] = img
        logits = inv_temp * lax.dot_general(img, txt, NT, preferred_element_type=F32)
        e = jnp.exp(logits)
        rowsum = jnp.sum(e, axis=1, keepdims=True)
        colsum = colsum + jnp.sum(e, axis=0, keepdims=True)
        rowsum_flat = rowsum_flat + jnp.sum(jnp.where(eye(r), rowsum, 0.0), axis=0, keepdims=True)
        diag = diag + jnp.sum(jnp.where(eye(r), logits, 0.0), axis=0, keepdims=True)
        invs.append(inv)
        es.append(e)
        rowsums.append(rowsum)

    half_col = 0.5 / colsum
    for r, inv, e, rowsum in zip(chunks, invs, es, rowsums):
        delta = e * (0.5 / rowsum + half_col) - jnp.where(eye(r), 1.0, 0.0)
        grad = jnp.dot(delta.astype(BF16), txt, preferred_element_type=F32)
        emb = emb_ref[r, :]
        along = jnp.sum(emb * grad, axis=1, keepdims=True) * (inv * inv)
        grad_s[r, :] = ((grad - emb * along) * (inv_temp * inv)).astype(BF16)

    rows = width // w_sem.shape[0]

    def abar(low, wide):
        for ref in (abar0, abar1, abar2):
            if low < ref.shape[1]:
                return ref[:, low : low + wide]
            low -= ref.shape[1]

    def w_copy(c):
        return pltpu.make_async_copy(
            w_s.at[pl.ds(c * rows, rows), :], w_hbm.at[pl.ds(c * rows, rows), :], w_sem.at[c]
        )

    for c in range(w_sem.shape[0]):
        w_s[c * rows : (c + 1) * rows, :] = lax.dot_general(
            abar(c * rows, rows), grad_s[...], TN, preferred_element_type=F32
        ).astype(BF16)
        w_copy(c).start()

    loss_ref[0, 0] = jnp.sum(
        jnp.log(rowsum_flat) + jnp.log(colsum) - 2.0 * diag
    ) / (2.0 * total)

    img = img_s[...]
    text32 = text_ref[...].astype(F32)
    txt_norm = jnp.sqrt(jnp.sum(text32 * text32, axis=1, keepdims=True) + epsilon)
    txt_f = text32 / txt_norm
    own = inv_temp * lax.dot_general(txt_f.astype(BF16), img, NT, preferred_element_type=F32)
    own_e = jnp.exp(own)
    own_sum = jnp.sum(own_e, axis=1, keepdims=True)
    col = lax.broadcasted_iota(jnp.int32, (images, total), 1)
    row = lax.broadcasted_iota(jnp.int32, (images, total), 0) + lax.axis_index("dp") * images
    own_delta = 0.5 * (own_e / rowsum_flat + own_e / own_sum) - jnp.where(col == row, 1.0, 0.0)
    grad_txt = inv_temp * jnp.dot(own_delta.astype(BF16), img, preferred_element_type=F32)
    text_grad_ref[...] = (
        grad_txt - txt_f * jnp.sum(txt_f * grad_txt, axis=1, keepdims=True)
    ) / txt_norm
    for c in range(w_sem.shape[0]):
        w_copy(c).wait()


def finish(all_txt, abars, emb, text_raw):
    images, width = text_raw.shape
    total = emb.shape[0]
    vmem = pl.BlockSpec(memory_space=pltpu.VMEM)
    smem = pl.BlockSpec(memory_space=pltpu.SMEM)
    loss, text_grad, w_grad = pl.pallas_call(
        loss_kernel,
        out_shape=(
            jax.ShapeDtypeStruct((1, 1), F32),
            jax.ShapeDtypeStruct((images, width), F32),
            jax.ShapeDtypeStruct((width, width), BF16),
        ),
        in_specs=[vmem] * 6,
        out_specs=(smem, vmem, pl.BlockSpec(memory_space=pl.ANY)),
        scratch_shapes=[
            pltpu.VMEM((total, width), BF16),
            pltpu.VMEM((total, width), BF16),
            pltpu.VMEM((width, width), BF16),
            pltpu.SemaphoreType.DMA((4,)),
        ],
        compiler_params=pltpu.CompilerParams(vmem_limit_bytes=40 * 2**20),
        name="finish",
    )(all_txt, *abars, emb, text_raw)
    return loss.reshape(()), text_grad, w_grad


def solution(mesh):
    n = mesh.shape["dp"]

    def local(features, ln_gain, w_query, w_key, w_value, w_out, text_raw):
        all_txt, *abars, emb, text = embed(
            features, ln_gain, w_query, w_key, w_value, w_out, text_raw, n
        )
        pairs = n * text_raw.shape[0]
        abars = [a.reshape(pairs, -1) for a in abars]
        return finish(all_txt.reshape(pairs, -1), abars, emb, text)

    placed = (P("dp", None, None), P(), P(), P(), P(), P(), P("dp", None))
    return jax.shard_map(
        local, mesh=mesh, in_specs=placed, out_specs=(P(), P("dp", None), P()), check_vma=False
    )
```

time: 36.8 us -> 28.7 us (0.78)
  Pallas kernels: 35.8 us -> 27.9 us
    pallas_call x1, Pallas kernels: 30.8 us -> 24.6 us  [embed(): pl.pallas_call(functools.partial(embed_kernel, n), out_shape=(pltpu.VMEM(...]
    pallas_call x1, Pallas kernels: 4.99 us -> 3.3 us  [finish(): pl.pallas_call(loss_kernel, out_shape=(jax.ShapeDtypeStruct((1, 1), F32),...]
where the time goes in v2:
time: 28.7 us; the launch traced here: 28.5 us
  Pallas kernels  27.9 us (97%)
  between operations  0.64 us (2%)
    pallas_call x1, Pallas kernels, embed(): pl.pallas_call(functools.partial(embed_kernel, n), out_shape=(pltpu.VMEM(...  24.6 us
    pallas_call x1, Pallas kernels, finish(): pl.pallas_call(loss_kernel, out_shape=(jax.ShapeDtypeStruct((1, 1), F32),...  3.3 us

profile of v2, /device:TPU:0, one launch (start us, length us, event | category | flops | bytes accessed | tf_op | source)
XLA Modules:
  0.0 28.5 jit_solution(2853208126395220302)
XLA Ops:
  0.6 24.6 %embed.1 = (bf16[32,8,1024]{2,1,0:T(8,128)(2,1)S(1)}, bf16[32,8,512]{2,1,0:T(8,128)(2,1)S(1)}, bf16[32,8,256]{2,1,0:T(8,128)(2,1)S(1)}, bf16[32,8,256]{2,1,0:T(8...) custom-call(bf16[8,128,1024]{2,1,0:T(8,128)(2,1)} %x_hbm.1, f32[1,1024]{1,0:T(1,128)} %bitcast.10, ...), custom_call_target="tpu_custom_call" | custom-call | tf_op jit(solution)/shard_map/embed/pallas_call | solution.py:392
  25.2 3.3 %finish.1 = (f32[1,1]{1,0:T(1,128)}, f32[8,1024]{1,0:T(8,128)}, bf16[1024,1024]{1,0:T(8,128)(2,1)}) custom-call(bf16[256,1024]{1,0:T(8,128)(2,1)S(1)} %bitcast.6, bf16[256,512]{1,0:T(8,128)(2,1)S(1)} %bitcast.7, bf16[256,256]{1,0:T(8,128)(2,1)S(1)} %bitcast.8, bf16[256,256]{1,0:T(8,128)(2,1)S(1)} %bitcast.9, f32[256,1024]{1,0:T(8,128)S(1)} %get-tuple-element.16.emb_ref, ...), custom_call_target="tpu_custom_call" | custom-call | tf_op jit(solution)/shard_map/finish/pallas_call | solution.py:515

commit v3 on v2

--- a/solution.py
+++ b/solution.py
@@ -37,13 +37,15 @@
 
 def greet(n):
     barrier = pltpu.get_barrier_semaphore()
+    me = lax.axis_index("dp")
 
     def hello(i, _):
-        pl.semaphore_signal(barrier, inc=1, device_id=(target(n, i),), device_id_type=MESH)
+        pl.semaphore_signal(
+            barrier, inc=1, device_id=(lax.rem(me + i, n),), device_id_type=MESH
+        )
         return 0
 
-    pl.semaphore_signal(barrier, inc=1, device_id=(mate(),), device_id_type=MESH)
-    lax.fori_loop(1, n // 2, hello, 0)
+    lax.fori_loop(1, n, hello, 0)
 
 
 def each(low, high, act):
@@ -106,6 +108,22 @@
     def start(self):
         own = self.own()
         each(1, self.half, lambda i: remote(own, own, self.sems, 0, target(self.n, i)).start())
+
+
+class Scatter(Exchange):
+    def start(self):
+        own = self.own()
+
+        def send(i):
+            remote(own, own, self.sems, 0, lax.rem(self.me + i, self.n)).start()
+
+        each(1, self.n, send)
+
+    def arrive(self):
+        self.several(0, self.n - 1).wait_recv()
+
+    def drain(self):
+        self.several(0, self.n - 1).wait_send()
 
 
 class LineShare(Exchange):
@@ -220,30 +238,30 @@
     gain = gain_ref[...]
     block = 32
 
+    def norm_block(i, b, acc):
+        x = xs[i, pl.ds(b * block, block), :].astype(F32)
+        center = x - jnp.mean(x, axis=-1, keepdims=True)
+        spread = jnp.mean(center * center, axis=-1, keepdims=True)
+        out = center * lax.rsqrt(spread + epsilon) * gain
+        rows = pl.ds(pl.multiple_of(i * tokens + b * block, block), block)
+        normed[rows, :] = out.astype(BF16)
+        return acc + jnp.sum(x, axis=0, keepdims=True)
+
+    def mean_tokens(i, total):
+        first = xs[i, pl.ds(0, 1), :].astype(F32)
+        xbar[pl.ds(i, 1), :] = first + (total - first) / (tokens - 1)
+
     def norm_image(i, _):
         x_copy(i).wait()
-
-        def norm_block(b, acc):
-            x = xs[i, pl.ds(b * block, block), :].astype(F32)
-            center = x - jnp.mean(x, axis=-1, keepdims=True)
-            spread = jnp.mean(center * center, axis=-1, keepdims=True)
-            out = center * lax.rsqrt(spread + epsilon) * gain
-            rows = pl.ds(pl.multiple_of(i * tokens + b * block, block), block)
-            normed[rows, :] = out.astype(BF16)
-            return acc + jnp.sum(x, axis=0, keepdims=True)
-
-        total = lax.fori_loop(0, tokens // block, norm_block, jnp.zeros((1, width), F32), unroll=4)
-        first = xs[i, pl.ds(0, 1), :].astype(F32)
-        xbar[pl.ds(i, 1), :] = first + (total - first) / (tokens - 1)
+        zero = jnp.zeros((1, width), F32)
+        total = lax.fori_loop(
+            0, tokens // block, lambda b, acc: norm_block(i, b, acc), zero, unroll=4
+        )
+        mean_tokens(i, total)
         return 0
 
-    lax.fori_loop(0, images, norm_image, 0)
-    all_xbar[me] = xbar[...].astype(BF16)
-    text_copy.wait()
-    text32 = text_ref[...].astype(F32)
-    txt_norm = jnp.sqrt(jnp.sum(text32 * text32, axis=1, keepdims=True) + epsilon)
-    all_txt[me] = (text32 / txt_norm).astype(BF16)
-
+    ahead = images // BLOCKS
+    lax.fori_loop(0, ahead, norm_image, 0)
     seg_row = lax.broadcasted_iota(jnp.int32, (cols, cols), 0) // head
     seg_col = lax.broadcasted_iota(jnp.int32, (cols, cols), 1) // head
     seg = jnp.where(seg_row == seg_col, 1.0, 0.0).astype(BF16)
@@ -319,23 +337,41 @@
         return jnp.concatenate(picked, axis=0).astype(BF16)
 
     early, late, last = groups // 2, groups - 1, groups
-    shares = [Share(n, part, share_sems.at[2 + c]) for c, part in enumerate(abars)]
+    kinds = (Share, Share, Scatter)
+    shares = [kinds[c](n, part, share_sems.at[2 + c]) for c, part in enumerate(abars)]
     for g in range(groups + 1):
         if g < groups:
             q_copy(g).wait()
             k_copy(g).wait()
         if g == 1:
-            pl.semaphore_wait(pltpu.get_barrier_semaphore(), n // 2)
+            pl.semaphore_wait(pltpu.get_barrier_semaphore(), n - 1)
+            xbar_share.start()
             txt_share.start()
-            xbar_share.start()
         if g == early + 1:
-            txt_share.spread()
             v_copy.wait()
             abars[0][me] = weigh(0, early)
             shares[0].start()
+            xbar_share.spread()
         if g == groups:
-            xbar_share.spread()
+            txt_share.spread()
             abars[1][me] = weigh(early, late)
+        if g == 0:
+            for i in range(ahead, images):
+                x_copy(i).wait()
+            for i in range(ahead, images):
+                total = jnp.zeros((1, width), F32)
+                for b in range(tokens // block):
+                    total = norm_block(i, b, total)
+                mean_tokens(i, total)
+            project(0, 0)
+            for b in range(1, BLOCKS):
+                project(0, b)
+            all_xbar[me] = xbar[...].astype(BF16)
+            text_copy.wait()
+            text32 = text_ref[...].astype(F32)
+            txt_norm = jnp.sqrt(jnp.sum(text32 * text32, axis=1, keepdims=True) + epsilon)
+            all_txt[me] = (text32 / txt_norm).astype(BF16)
+            continue
         for b in range(BLOCKS):
             if g > 0:
                 for i in range(b * images // BLOCKS, (b + 1) * images // BLOCKS):
@@ -345,12 +381,10 @@
     shares[1].start()
     abars[2][me] = weigh(late, last)
     shares[2].start()
-    txt_share.forward()
     xbar_share.forward()
     shares[0].forward()
     shares[1].forward()
-    xbar_share.arrive()
-    shares[0].arrive()
+    txt_share.forward()
     o_copy.wait()
 
     total = n * images
@@ -364,21 +398,21 @@
         w = wos[low * cols : high * cols, :]
         return jnp.dot(join(abars[c], r), w, preferred_element_type=F32)
 
+    for share in (xbar_share, shares[0]):
+        share.arrive()
+        share.drain()
     for r in range(total // chunk):
         emb = join(all_xbar, r).astype(F32) + out_part(r, 0, 0, early)
         emb_ref[r * chunk : (r + 1) * chunk, :] = emb
-    shares[2].forward()
-    txt_share.arrive()
-    shares[1].arrive()
-    for share in (txt_share, xbar_share, *shares):
-        if share is not shares[2]:
-            share.drain()
-    shares[2].arrive()
+    for share in (shares[1], shares[2]):
+        share.arrive()
     for r in range(total // chunk):
         emb_ref[r * chunk : (r + 1) * chunk, :] += out_part(r, 1, early, late) + out_part(
             r, 2, late, last
         )
-    shares[2].drain()
+    txt_share.arrive()
+    for share in (txt_share, shares[1], shares[2]):
+        share.drain()
 
 
 def embed(features, ln_gain, w_query, w_key, w_value, w_out, text_raw, n):
@@ -428,16 +462,46 @@
 
 
 def loss_kernel(
-    txt_ref, abar0, abar1, abar2, emb_ref, text_ref, loss_ref, text_grad_ref, w_hbm, img_s, grad_s, w_s, w_sem
+    txt_ref,
+    abar0,
+    abar1,
+    abar2,
+    emb_ref,
+    text_ref,
+    loss_hbm,
+    text_grad_hbm,
+    w_hbm,
+    img_s,
+    grad_s,
+    w_s,
+    loss_s,
+    text_grad_s,
+    out_sem,
 ):
     total, width = emb_ref.shape
     images = text_ref.shape[0]
     chunk = min(total, 256)
     chunks = [slice(r, r + chunk) for r in range(0, total, chunk)]
+    pieces = 4
+    rows = width // pieces
+
+    def w_copy(c):
+        return pltpu.make_async_copy(
+            w_s.at[pl.ds(c * rows, rows), :], w_hbm.at[pl.ds(c * rows, rows), :], out_sem.at[c]
+        )
+
+    loss_copy = pltpu.make_async_copy(loss_s, loss_hbm, out_sem.at[pieces])
+    text_copy = pltpu.make_async_copy(text_grad_s, text_grad_hbm, out_sem.at[pieces + 1])
 
     def eye(r):
         row = lax.broadcasted_iota(jnp.int32, (chunk, total), 0) + r.start
         return row == lax.broadcasted_iota(jnp.int32, (chunk, total), 1)
+
+    def abar(low, wide):
+        for ref in (abar0, abar1, abar2):
+            if low < ref.shape[1]:
+                return ref[:, low : low + wide]
+            low -= ref.shape[1]
 
     txt = txt_ref[...]
     invs, es, rowsums = [], [], []
@@ -459,6 +523,12 @@
         rowsums.append(rowsum)
 
     half_col = 0.5 / colsum
+    text32 = text_ref[...].astype(F32)
+    txt_norm = jnp.sqrt(jnp.sum(text32 * text32, axis=1, keepdims=True) + epsilon)
+    txt_f = text32 / txt_norm
+    img = img_s[...]
+    own = inv_temp * lax.dot_general(txt_f.astype(BF16), img, NT, preferred_element_type=F32)
+
     for r, inv, e, rowsum in zip(chunks, invs, es, rowsums):
         delta = e * (0.5 / rowsum + half_col) - jnp.where(eye(r), 1.0, 0.0)
         grad = jnp.dot(delta.astype(BF16), txt, preferred_element_type=F32)
@@ -466,52 +536,37 @@
         along = jnp.sum(emb * grad, axis=1, keepdims=True) * (inv * inv)
         grad_s[r, :] = ((grad - emb * along) * (inv_temp * inv)).astype(BF16)
 
-    rows = width // w_sem.shape[0]
-
-    def abar(low, wide):
-        for ref in (abar0, abar1, abar2):
-            if low < ref.shape[1]:
-                return ref[:, low : low + wide]
-            low -= ref.shape[1]
-
-    def w_copy(c):
-        return pltpu.make_async_copy(
-            w_s.at[pl.ds(c * rows, rows), :], w_hbm.at[pl.ds(c * rows, rows), :], w_sem.at[c]
-        )
-
-    for c in range(w_sem.shape[0]):
-        w_s[c * rows : (c + 1) * rows, :] = lax.dot_general(
-            abar(c * rows, rows), grad_s[...], TN, preferred_element_type=F32
-        ).astype(BF16)
-        w_copy(c).start()
-
-    loss_ref[0, 0] = jnp.sum(
-        jnp.log(rowsum_flat) + jnp.log(colsum) - 2.0 * diag
-    ) / (2.0 * total)
-
-    img = img_s[...]
-    text32 = text_ref[...].astype(F32)
-    txt_norm = jnp.sqrt(jnp.sum(text32 * text32, axis=1, keepdims=True) + epsilon)
-    txt_f = text32 / txt_norm
-    own = inv_temp * lax.dot_general(txt_f.astype(BF16), img, NT, preferred_element_type=F32)
+    loss = jnp.sum(jnp.log(rowsum_flat) + jnp.log(colsum) - 2.0 * diag, axis=1, keepdims=True)
+    loss_s[...] = loss / (2.0 * total)
     own_e = jnp.exp(own)
     own_sum = jnp.sum(own_e, axis=1, keepdims=True)
     col = lax.broadcasted_iota(jnp.int32, (images, total), 1)
     row = lax.broadcasted_iota(jnp.int32, (images, total), 0) + lax.axis_index("dp") * images
     own_delta = 0.5 * (own_e / rowsum_flat + own_e / own_sum) - jnp.where(col == row, 1.0, 0.0)
     grad_txt = inv_temp * jnp.dot(own_delta.astype(BF16), img, preferred_element_type=F32)
-    text_grad_ref[...] = (
+    text_grad_s[...] = (
         grad_txt - txt_f * jnp.sum(txt_f * grad_txt, axis=1, keepdims=True)
     ) / txt_norm
-    for c in range(w_sem.shape[0]):
+
+    for c in range(pieces):
+        w_s[c * rows : (c + 1) * rows, :] = lax.dot_general(
+            abar(c * rows, rows), grad_s[...], TN, preferred_element_type=F32
+        ).astype(BF16)
+        w_copy(c).start()
+        if c == 0:
+            loss_copy.start()
+            text_copy.start()
+    for c in range(pieces):
         w_copy(c).wait()
+    loss_copy.wait()
+    text_copy.wait()
 
 
 def finish(all_txt, abars, emb, text_raw):
     images, width = text_raw.shape
     total = emb.shape[0]
     vmem = pl.BlockSpec(memory_space=pltpu.VMEM)
-    smem = pl.BlockSpec(memory_space=pltpu.SMEM)
+    hbm = pl.BlockSpec(memory_space=pl.ANY)
     loss, text_grad, w_grad = pl.pallas_call(
         loss_kernel,
         out_shape=(
@@ -520,12 +575,14 @@
             jax.ShapeDtypeStruct((width, width), BF16),
         ),
         in_specs=[vmem] * 6,
-        out_specs=(smem, vmem, pl.BlockSpec(memory_space=pl.ANY)),
+        out_specs=(hbm,) * 3,
         scratch_shapes=[
             pltpu.VMEM((total, width), BF16),
             pltpu.VMEM((total, width), BF16),
             pltpu.VMEM((width, width), BF16),
-            pltpu.SemaphoreType.DMA((4,)),
+            pltpu.VMEM((1, 1), F32),
+            pltpu.VMEM((images, width), F32),
+            pltpu.SemaphoreType.DMA((6,)),
         ],
         compiler_params=pltpu.CompilerParams(vmem_limit_bytes=40 * 2**20),
         name="finish",

time: 28.7 us -> 26.6 us (0.927)
  Pallas kernels: 27.9 us -> 25.6 us
    pallas_call x1, Pallas kernels: 24.6 us -> 22.9 us  [embed(): pl.pallas_call(functools.partial(embed_kernel, n), out_shape=(pltpu.VMEM(...]
    pallas_call x1, Pallas kernels: 3.3 us -> 2.65 us  [finish(): pl.pallas_call(loss_kernel, out_shape=(jax.ShapeDtypeStruct((1, 1), F32),...]
where the time goes in v3:
time: 26.6 us; the launch traced here: 26.4 us
  Pallas kernels  25.6 us (96%)
  between operations  0.8 us (3%)
    pallas_call x1, Pallas kernels, embed(): pl.pallas_call(functools.partial(embed_kernel, n), out_shape=(pltpu.VMEM(...  22.9 us
    pallas_call x1, Pallas kernels, finish(): pl.pallas_call(loss_kernel, out_shape=(jax.ShapeDtypeStruct((1, 1), F32),...  2.65 us

profile of v3, /device:TPU:0, one launch (start us, length us, event | category | flops | bytes accessed | tf_op | source)
XLA Modules:
  0.0 26.4 jit_solution(91613479495133126)
XLA Ops:
  0.6 22.9 %embed.1 = (bf16[32,8,1024]{2,1,0:T(8,128)(2,1)S(1)}, bf16[32,8,512]{2,1,0:T(8,128)(2,1)S(1)}, bf16[32,8,256]{2,1,0:T(8,128)(2,1)S(1)}, bf16[32,8,256]{2,1,0:T(8...) custom-call(bf16[8,128,1024]{2,1,0:T(8,128)(2,1)} %x_hbm.1, f32[1,1024]{1,0:T(1,128)} %bitcast.10, ...), custom_call_target="tpu_custom_call" | custom-call | tf_op jit(solution)/shard_map/embed/pallas_call | solution.py:426
  23.6 2.7 %finish.1 = (f32[1,1]{1,0:T(1,128)}, f32[8,1024]{1,0:T(8,128)}, bf16[1024,1024]{1,0:T(8,128)(2,1)}) custom-call(bf16[256,1024]{1,0:T(8,128)(2,1)S(1)} %bitcast.6, bf16[256,512]{1,0:T(8,128)(2,1)S(1)} %bitcast.7, bf16[256,256]{1,0:T(8,128)(2,1)S(1)} %bitcast.8, bf16[256,256]{1,0:T(8,128)(2,1)S(1)} %bitcast.9, f32[256,1024]{1,0:T(8,128)S(1)} %get-tuple-element.16.emb_ref, ...), custom_call_target="tpu_custom_call" | custom-call | tf_op jit(solution)/shard_map/finish/pallas_call | solution.py:570

commit v4 on v3

--- a/solution.py
+++ b/solution.py
@@ -48,12 +48,12 @@
     lax.fori_loop(1, n, hello, 0)
 
 
-def each(low, high, act):
+def each(low, high, act, unroll=1):
     def step(i, _):
         act(i)
         return 0
 
-    lax.fori_loop(low, high, step, 0)
+    lax.fori_loop(low, high, step, 0, unroll=unroll)
 
 
 def remote(src, dst, sems, kind, device):
@@ -72,6 +72,7 @@
         self.n, self.ref, self.sems = n, ref, sems
         self.me = lax.axis_index("dp")
         self.half = n // 2
+        self.parity = lax.rem(self.me, 2)
 
     def own(self):
         return self.ref.at[self.me]
@@ -81,8 +82,7 @@
         return remote(blocks, blocks, self.sems, kind, mate())
 
     def relay(self):
-        parity = lax.rem(self.me, 2)
-        blocks = self.ref.reshape(self.half, 2, *self.ref.shape[1:]).at[:, parity]
+        blocks = self.ref.reshape(self.half, 2, *self.ref.shape[1:]).at[:, self.parity]
         return remote(blocks, blocks, self.sems, self.last, mate())
 
     def forward(self):
@@ -101,23 +101,34 @@
 class Share(Exchange):
     last = 1
 
-    def __init__(self, n, ref, sems):
+    def __init__(self, n, ref, sems, own):
         super().__init__(n, ref, sems)
-        self.counts = ((0, self.half - 1),)
+        self.counts = ((0, self.half),)
+        self.source = own
+        self.parity = 1 - lax.rem(self.me, 2)
 
     def start(self):
-        own = self.own()
-        each(1, self.half, lambda i: remote(own, own, self.sems, 0, target(self.n, i)).start())
+        def send(i):
+            device = target(self.n, i)
+            device = device + 1 - 2 * lax.rem(device, 2)
+            remote(self.source, self.own(), self.sems, 0, device).start()
+
+        each(0, self.half, send)
 
 
 class Scatter(Exchange):
     def start(self):
         own = self.own()
+        turn = 2 * (self.me // self.half) - 1
 
         def send(i):
-            remote(own, own, self.sems, 0, lax.rem(self.me + i, self.n)).start()
-
-        each(1, self.n, send)
+            device = lax.rem(self.me + turn * i + self.n, self.n)
+            remote(own, own, self.sems, 0, device).start()
+
+        first = 1 + (self.n - 1) % 4
+        for i in range(1, first):
+            send(i)
+        each(first, self.n, send, unroll=4)
 
     def arrive(self):
         self.several(0, self.n - 1).wait_recv()
@@ -193,6 +204,9 @@
     q_sem,
     k_sem,
     w_sem,
+    own0,
+    own1,
+    vs,
     share_sems,
 ):
     images, tokens, width = xs.shape
@@ -336,9 +350,34 @@
         ]
         return jnp.concatenate(picked, axis=0).astype(BF16)
 
+    def value(b):
+        rows = pl.ds(b * (images * tokens // BLOCKS), images * tokens // BLOCKS)
+        wv = wvs[:, width - cols : width]
+        vs[rows, :] = jnp.dot(normed[rows, :], wv, preferred_element_type=F32).astype(BF16)
+
+    def weigh_last():
+        slot = lax.broadcasted_iota(jnp.int32, (2 * SLOTS, cols), 0)
+        owner = lax.broadcasted_iota(jnp.int32, (2 * SLOTS, cols), 1) // head
+        keep = lax.rem(slot, SLOTS) == owner
+        picked = []
+        for i in range(images):
+            p = pooled[i, (groups - 1) * SLOTS : groups * SLOTS, :]
+            hi = p.astype(BF16)
+            lo = (p - hi.astype(F32)).astype(BF16)
+            full = jnp.dot(
+                jnp.concatenate([hi, lo], axis=0),
+                vs[i * tokens : (i + 1) * tokens, :],
+                preferred_element_type=F32,
+            )
+            picked.append(jnp.sum(jnp.where(keep, full, 0.0), axis=0, keepdims=True))
+        return jnp.concatenate(picked, axis=0).astype(BF16)
+
     early, late, last = groups // 2, groups - 1, groups
-    kinds = (Share, Share, Scatter)
-    shares = [kinds[c](n, part, share_sems.at[2 + c]) for c, part in enumerate(abars)]
+    shares = [
+        Share(n, abar0, share_sems.at[2], own0),
+        Share(n, abar1, share_sems.at[3], own1),
+        Scatter(n, abar2, share_sems.at[4]),
+    ]
     for g in range(groups + 1):
         if g < groups:
             q_copy(g).wait()
@@ -349,12 +388,13 @@
             txt_share.start()
         if g == early + 1:
             v_copy.wait()
-            abars[0][me] = weigh(0, early)
+            own0[...] = weigh(0, early)
             shares[0].start()
             xbar_share.spread()
         if g == groups:
+            own1[...] = weigh(early, late)
+            shares[1].start()
             txt_share.spread()
-            abars[1][me] = weigh(early, late)
         if g == 0:
             for i in range(ahead, images):
                 x_copy(i).wait()
@@ -373,13 +413,14 @@
             all_txt[me] = (text32 / txt_norm).astype(BF16)
             continue
         for b in range(BLOCKS):
+            if g == groups:
+                value(b)
             if g > 0:
                 for i in range(b * images // BLOCKS, (b + 1) * images // BLOCKS):
                     attend(g - 1, i)
             if g < groups:
                 project(g, b)
-    shares[1].start()
-    abars[2][me] = weigh(late, last)
+    abars[2][me] = weigh_last()
     shares[2].start()
     xbar_share.forward()
     shares[0].forward()
@@ -398,20 +439,17 @@
         w = wos[low * cols : high * cols, :]
         return jnp.dot(join(abars[c], r), w, preferred_element_type=F32)
 
-    for share in (xbar_share, shares[0]):
+    for share in (xbar_share, *shares[:2]):
         share.arrive()
         share.drain()
     for r in range(total // chunk):
-        emb = join(all_xbar, r).astype(F32) + out_part(r, 0, 0, early)
+        emb = join(all_xbar, r).astype(F32) + out_part(r, 0, 0, early) + out_part(r, 1, early, late)
         emb_ref[r * chunk : (r + 1) * chunk, :] = emb
-    for share in (shares[1], shares[2]):
-        share.arrive()
+    shares[2].arrive()
     for r in range(total // chunk):
-        emb_ref[r * chunk : (r + 1) * chunk, :] += out_part(r, 1, early, late) + out_part(
-            r, 2, late, last
-        )
+        emb_ref[r * chunk : (r + 1) * chunk, :] += out_part(r, 2, late, last)
     txt_share.arrive()
-    for share in (txt_share, shares[1], shares[2]):
+    for share in (txt_share, shares[2]):
         share.drain()
 
 
@@ -452,6 +490,9 @@
             pltpu.SemaphoreType.DMA((groups,)),
             pltpu.SemaphoreType.DMA((groups,)),
             pltpu.SemaphoreType.DMA((4,)),
+            pltpu.VMEM((images, width // 2), BF16),
+            pltpu.VMEM((images, width // 4), BF16),
+            pltpu.VMEM((images * tokens, cols), BF16),
             pltpu.SemaphoreType.DMA((5, 6)),
         ],
         compiler_params=pltpu.CompilerParams(

time: 26.6 us -> 26.1 us (0.981)
  Pallas kernels: 25.6 us -> 25.3 us
    pallas_call x1, Pallas kernels: 22.9 us -> 22.6 us  [embed(): pl.pallas_call(functools.partial(embed_kernel, n), out_shape=(pltpu.VMEM(...]
where the time goes in v4:
time: 26.1 us; the launch traced here: 25.9 us
  Pallas kernels  25.3 us (97%)
  between operations  0.64 us (2%)
    pallas_call x1, Pallas kernels, embed(): pl.pallas_call(functools.partial(embed_kernel, n), out_shape=(pltpu.VMEM(...  22.6 us
    pallas_call x1, Pallas kernels, finish(): pl.pallas_call(loss_kernel, out_shape=(jax.ShapeDtypeStruct((1, 1), F32),...  2.65 us

profile of v4, /device:TPU:0, one launch (start us, length us, event | category | flops | bytes accessed | tf_op | source)
XLA Modules:
  0.0 25.9 jit_solution(8124931729962053110)
XLA Ops:
  0.6 22.6 %embed.1 = (bf16[32,8,1024]{2,1,0:T(8,128)(2,1)S(1)}, bf16[32,8,512]{2,1,0:T(8,128)(2,1)S(1)}, bf16[32,8,256]{2,1,0:T(8,128)(2,1)S(1)}, bf16[32,8,256]{2,1,0:T(8...) custom-call(bf16[8,128,1024]{2,1,0:T(8,128)(2,1)} %x_hbm.1, f32[1,1024]{1,0:T(1,128)} %bitcast.10, ...), custom_call_target="tpu_custom_call" | custom-call | tf_op jit(solution)/shard_map/embed/pallas_call | solution.py:464
  23.3 2.6 %finish.1 = (f32[1,1]{1,0:T(1,128)}, f32[8,1024]{1,0:T(8,128)}, bf16[1024,1024]{1,0:T(8,128)(2,1)}) custom-call(bf16[256,1024]{1,0:T(8,128)(2,1)S(1)} %bitcast.6, bf16[256,512]{1,0:T(8,128)(2,1)S(1)} %bitcast.7, bf16[256,256]{1,0:T(8,128)(2,1)S(1)} %bitcast.8, bf16[256,256]{1,0:T(8,128)(2,1)S(1)} %bitcast.9, f32[256,1024]{1,0:T(8,128)S(1)} %get-tuple-element.16.emb_ref, ...), custom_call_target="tpu_custom_call" | custom-call | tf_op jit(solution)/shard_map/finish/pallas_call | solution.py:611

commit v5 on v4

--- a/solution.py
+++ b/solution.py
@@ -207,7 +207,11 @@
     own0,
     own1,
     vs,
-    share_sems,
+    xbar_sems,
+    txt_sems,
+    sems0,
+    sems1,
+    sems2,
 ):
     images, tokens, width = xs.shape
     groups = wqks.shape[0]
@@ -244,8 +248,8 @@
     v_copy.start()
     o_copy.start()
 
-    txt_share = LineShare(n, all_txt, share_sems.at[0])
-    xbar_share = LineShare(n, all_xbar, share_sems.at[1])
+    txt_share = LineShare(n, all_txt, txt_sems)
+    xbar_share = LineShare(n, all_xbar, xbar_sems)
 
     pooled[...] = jnp.zeros_like(pooled)
     gain_copy.wait()
@@ -374,9 +378,9 @@
 
     early, late, last = groups // 2, groups - 1, groups
     shares = [
-        Share(n, abar0, share_sems.at[2], own0),
-        Share(n, abar1, share_sems.at[3], own1),
-        Scatter(n, abar2, share_sems.at[4]),
+        Share(n, abar0, sems0, own0),
+        Share(n, abar1, sems1, own1),
+        Scatter(n, abar2, sems2),
     ]
     for g in range(groups + 1):
         if g < groups:
@@ -493,7 +497,11 @@
             pltpu.VMEM((images, width // 2), BF16),
             pltpu.VMEM((images, width // 4), BF16),
             pltpu.VMEM((images * tokens, cols), BF16),
-            pltpu.SemaphoreType.DMA((5, 6)),
+            pltpu.SemaphoreType.DMA((6,)),
+            pltpu.SemaphoreType.DMA((6,)),
+            pltpu.SemaphoreType.DMA((4,)),
+            pltpu.SemaphoreType.DMA((4,)),
+            pltpu.SemaphoreType.DMA((2,)),
         ],
         compiler_params=pltpu.CompilerParams(
             collective_id=0, has_side_effects=True, vmem_limit_bytes=40 * 2**20

time: 26.1 us -> 26 us (level)
  no operation moved by 1% of the time
where the time goes in v5:
time: 26 us; the launch traced here: 25.8 us
  Pallas kernels  25.2 us (97%)
  between operations  0.64 us (2%)
    pallas_call x1, Pallas kernels, embed(): pl.pallas_call(functools.partial(embed_kernel, n), out_shape=(pltpu.VMEM(...  22.5 us
    pallas_call x1, Pallas kernels, finish(): pl.pallas_call(loss_kernel, out_shape=(jax.ShapeDtypeStruct((1, 1), F32),...  2.65 us

profile of v5, /device:TPU:0, one launch (start us, length us, event | category | flops | bytes accessed | tf_op | source)
XLA Modules:
  0.0 25.8 jit_solution(7561068601679922724)
XLA Ops:
  0.6 22.5 %embed.1 = (bf16[32,8,1024]{2,1,0:T(8,128)(2,1)S(1)}, bf16[32,8,512]{2,1,0:T(8,128)(2,1)S(1)}, bf16[32,8,256]{2,1,0:T(8,128)(2,1)S(1)}, bf16[32,8,256]{2,1,0:T(8...) custom-call(bf16[8,128,1024]{2,1,0:T(8,128)(2,1)} %x_hbm.1, f32[1,1024]{1,0:T(1,128)} %bitcast.10, ...), custom_call_target="tpu_custom_call" | custom-call | tf_op jit(solution)/shard_map/embed/pallas_call | solution.py:468
  23.2 2.6 %finish.1 = (f32[1,1]{1,0:T(1,128)}, f32[8,1024]{1,0:T(8,128)}, bf16[1024,1024]{1,0:T(8,128)(2,1)}) custom-call(bf16[256,1024]{1,0:T(8,128)(2,1)S(1)} %bitcast.6, bf16[256,512]{1,0:T(8,128)(2,1)S(1)} %bitcast.7, bf16[256,256]{1,0:T(8,128)(2,1)S(1)} %bitcast.8, bf16[256,256]{1,0:T(8,128)(2,1)S(1)} %bitcast.9, f32[256,1024]{1,0:T(8,128)S(1)} %get-tuple-element.16.emb_ref, ...), custom_call_target="tpu_custom_call" | custom-call | tf_op jit(solution)/shard_map/finish/pallas_call | solution.py:619
